TPU v7x, 256 devices: a whole 4x4x8 slice. The times are simulated.
256 devices in a mesh: slab: 64 (over z, y, core), pencil: 4 (over x).
Axes of the slice: x: 4, y: 4, z: 8, core: 2. Of those that a mesh axis runs over, the one named last changes fastest.
Arguments:
- density_history: float32 [7, 512, 320, 320], P(None, 'slab', 'pencil'), may hold values from -6 to 6
- residual_history: float32 [7, 512, 320, 320], P(None, 'slab', 'pencil'), as said below
- occupancy_history: float32 [7, 6144, 324], P(None, ('slab', 'pencil')), may hold values from -6 to 6
- occupancy_residual: float32 [7, 6144, 324], P(None, ('slab', 'pencil')), may hold values from -6 to 6
- species: int32 [6144], P(('slab', 'pencil')), may hold values from 0 to 3
- slot_count: int32 [256], P(('slab', 'pencil')), may hold values from 12 to 24, as said below
Outputs:
- new_density: float32 [512, 320, 320], P('slab', 'pencil')
- new_occupancy: float32 [6144, 324], P(('slab', 'pencil'))
Inputs may be any that keep to these rules, and one draw needn't show every extreme that they name: `residual_history`: residual fields of the 7 previous steps. Device d of slab+pencil (slab slowest) holds slots d * 24 to (d + 1) * 24 - 1, of which the first slot_count[d] hold atoms; some device is full in every draw.
All inputs are finite; a program needn't handle non-finite values.
Results may differ from a plain program's by a relative error of at most 0.00017.
Values sent between devices are 32-bit elements; how exact they have to be, the bound alone decides.
A program may use at most 128 MiB of HBM per device.

v0:
```python
import functools
import math

import numpy as np

import jax
import jax.numpy as jnp
from jax import lax
from jax.experimental import pallas as pl
from jax.experimental.pallas import tpu as pltpu
from jax.sharding import Mesh
from jax.sharding import PartitionSpec as P

ORBITALS = 18
SLAB = ("slab_0", "slab_1", "slab_2")
SLAB_PENCIL = ("slab_0", "slab_1", "slab_2", "pencil")

grid_mixing = 0.5
block_mixing = 0.5
kerker_wave = 6.0
species_orbitals = (18, 13, 8, 5)


def real_basis(length):
    half = length // 2
    n = np.arange(length)
    rows = [np.full(length, 1.0 / math.sqrt(length))]
    waves = [0]
    for k in range(1, half):
        angle = 2.0 * math.pi * ((k * n) % length) / length
        rows.append(math.sqrt(2.0 / length) * np.cos(angle))
        rows.append(math.sqrt(2.0 / length) * np.sin(angle))
        waves += [k, k]
    rows.append(np.where(n % 2 == 0, 1.0, -1.0) / math.sqrt(length))
    waves.append(half)
    return np.stack(rows).astype(np.float32), np.array(waves, np.float32)


def block_mask(species, slot_count):
    live = jnp.arange(species.shape[0], dtype=jnp.int32) < slot_count[0]
    orbitals = jnp.zeros_like(species)
    for species_index, orbital_number in enumerate(species_orbitals):
        orbitals = orbitals + orbital_number * (species == species_index).astype(jnp.int32)
    entry = jnp.arange(ORBITALS * ORBITALS, dtype=jnp.int32)
    row_index = entry // ORBITALS
    column_index = entry % ORBITALS
    inside = (
        (row_index[None, :] < orbitals[:, None])
        & (column_index[None, :] < orbitals[:, None])
        & live[:, None]
    )
    return inside.astype(jnp.float32)


def mixing_weights(intersection):
    factor = jnp.linalg.cholesky(intersection)
    column = jnp.ones((intersection.shape[0], 1), intersection.dtype)
    middle = lax.linalg.triangular_solve(factor, column, left_side=True, lower=True)
    solved = lax.linalg.triangular_solve(
        factor, middle, left_side=True, lower=True, transpose_a=True
    )
    return solved[:, 0] / jnp.sum(solved)


def gram_kernel(history, pairs, field_ref, out_ref):
    rows = field_ref.shape[2]

    def step(r, acc):
        at = pl.multiple_of(r * 8, 8)
        acc = list(acc)
        for lanes in ((0, 128), (128, 128)):
            v = [field_ref[i, 0, pl.ds(at, 8), lanes[0] : lanes[0] + lanes[1]] for i in range(history)]
            for n, (i, j) in enumerate(pairs):
                acc[n] = acc[n] + v[i] * v[j]
        v = [field_ref[i, 0, pl.ds(at, 8), 256:320] for i in range(history)]
        v = [jnp.concatenate([x, jnp.zeros_like(x)], axis=1) for x in v]
        for n, (i, j) in enumerate(pairs):
            acc[n] = acc[n] + v[i] * v[j]
        return tuple(acc)

    zero = jnp.zeros((8, 128), jnp.float32)
    acc = lax.fori_loop(0, rows // 8, step, (zero,) * len(pairs))

    @pl.when(pl.program_id(0) == 0)
    def _():
        for n in range(len(pairs)):
            out_ref[n] = acc[n]

    @pl.when(pl.program_id(0) > 0)
    def _():
        for n in range(len(pairs)):
            out_ref[n] += acc[n]


def gram_partial(field):
    history, planes, rows, columns = field.shape
    pairs = [(i, j) for i in range(history) for j in range(i + 1)]
    out = pl.pallas_call(
        functools.partial(gram_kernel, history, pairs),
        grid=(planes,),
        in_specs=[pl.BlockSpec((history, 1, rows, columns), lambda z: (0, z, 0, 0))],
        out_specs=pl.BlockSpec((len(pairs), 8, 128), lambda z: (0, 0, 0)),
        out_shape=jax.ShapeDtypeStruct((len(pairs), 8, 128), jnp.float32),
    )(field)
    flat = jnp.sum(out, axis=(1, 2))
    index = np.zeros((history, history), np.int32)
    for n, (i, j) in enumerate(pairs):
        index[i, j] = index[j, i] = n
    select = np.zeros((history * history, len(pairs)), np.float32)
    select[np.arange(history * history), index.reshape(-1)] = 1.0
    return jnp.sum(select * flat[None, :], axis=1).reshape(history, history)


def mix_kernel(history, weights_ref, field_ref, *rest):
    out_ref = rest[-1]
    total = weights_ref[0] * field_ref[0]
    for i in range(1, history):
        total += weights_ref[i] * field_ref[i]
    if len(rest) == 2:
        total += grid_mixing * rest[0][...]
    out_ref[...] = total


def mix(weights, field, extra=None):
    history, planes, rows, columns = field.shape
    plane = pl.BlockSpec((1, rows, columns), lambda z: (z, 0, 0))
    args = (weights, field) + (() if extra is None else (extra,))
    return pl.pallas_call(
        functools.partial(mix_kernel, history),
        grid=(planes,),
        in_specs=[
            pl.BlockSpec(memory_space=pltpu.SMEM),
            pl.BlockSpec((history, 1, rows, columns), lambda z: (0, z, 0, 0)),
        ]
        + [plane] * (len(args) - 2),
        out_specs=plane,
        out_shape=jax.ShapeDtypeStruct((planes, rows, columns), jnp.float32),
    )(*args)


def body(
    density_history, residual_history, occupancy_history, occupancy_residual, species, slot_count
):
    histories, z_local, y_local, x_length = residual_history.shape
    slabs = lax.axis_size(SLAB)
    pencils = lax.axis_size("pencil")
    y_length = y_local * pencils
    z_length = z_local * slabs
    kx_local = x_length // pencils
    ky_local = y_length // slabs
    cells = z_length * y_length * x_length
    slot_total = species.shape[0] * slabs * pencils
    mask = block_mask(species, slot_count)
    grid_local = gram_partial(residual_history) / cells
    blocks = occupancy_residual * mask[None]
    block_local = jnp.sum(blocks[:, None] * blocks[None, :], axis=(2, 3)) / (100.0 * slot_total)
    weights = mixing_weights(lax.psum(grid_local + block_local, SLAB_PENCIL))
    mixed = mix(weights, residual_history)

    high = lax.Precision.HIGH
    qx, wx = real_basis(x_length)
    qy, wy = real_basis(y_length)
    qz, wz = real_basis(z_length)
    h = jnp.einsum("kx,zyx->kzy", qx, mixed, precision=high).reshape(pencils, -1)
    h = lax.all_to_all(h, "pencil", split_axis=0, concat_axis=0, tiled=True)
    h = h.reshape(pencils, kx_local, z_local, y_local)
    h = jnp.einsum("lqy,qkzy->lkz", qy.reshape(y_length, pencils, y_local), h, precision=high)
    h = lax.all_to_all(h.reshape(slabs, -1), SLAB, split_axis=0, concat_axis=0, tiled=True)
    h = h.reshape(slabs, ky_local, kx_local, z_local)
    qz3 = qz.reshape(z_length, slabs, z_local)
    h = jnp.einsum("msz,slkz->mlk", qz3, h, precision=high)
    own_x = lax.dynamic_slice_in_dim(jnp.asarray(wx), lax.axis_index("pencil") * kx_local, kx_local)
    own_y = lax.dynamic_slice_in_dim(jnp.asarray(wy), lax.axis_index(SLAB) * ky_local, ky_local)
    square = (wz**2)[:, None, None] + (own_y**2)[None, :, None] + (own_x**2)[None, None, :]
    h = h * (square / (square + kerker_wave * kerker_wave))
    h = jnp.einsum("msz,mlk->slkz", qz3, h, precision=high)
    h = lax.all_to_all(h.reshape(slabs, -1), SLAB, split_axis=0, concat_axis=0, tiled=True)
    h = h.reshape(y_length, kx_local, z_local)
    h = jnp.einsum("lqy,lkz->qkzy", qy.reshape(y_length, pencils, y_local), h, precision=high)
    h = lax.all_to_all(h.reshape(pencils, -1), "pencil", split_axis=0, concat_axis=0, tiled=True)
    h = h.reshape(x_length, z_local, y_local)
    filtered = jnp.einsum("kx,kzy->zyx", qx, h, precision=high)
    new_density = mix(weights, density_history, filtered)
    mixed_blocks = jnp.sum(
        weights[:, None, None] * (occupancy_history + block_mixing * occupancy_residual), axis=0
    )
    return (new_density, mask * mixed_blocks)


def solution(mesh):
    torus = Mesh(
        mesh.devices.reshape(8, 4, 2, mesh.shape["pencil"]),
        ("slab_0", "slab_1", "slab_2", "pencil"),
    )
    placed = (
        P(None, SLAB, "pencil", None),
        P(None, SLAB, "pencil", None),
        P(None, SLAB_PENCIL, None),
        P(None, SLAB_PENCIL, None),
        P(SLAB_PENCIL),
        P(SLAB_PENCIL),
    )
    return jax.shard_map(
        body,
        mesh=torus,
        in_specs=placed,
        out_specs=(P(SLAB, "pencil", None), P(SLAB_PENCIL, None)),
        check_vma=False,
    )
```

profile of v0, /device:TPU:1, one launch (start us, length us, event | category | flops | bytes accessed | tf_op | source)
XLA Modules:
  0.0 281.5 jit_solution(11327492705469618759)
XLA Ops:
  2.0 1.0 broadcast_multiply_fusion
  3.4 7.3 %shard_map.167 = f32[28,8,128]{2,1,0:T(8,128)} custom-call(f32[7,8,80,320]{3,2,1,0:T(8,128)} %field_ref.4), custom_call_target="tpu_custom_call" | custom-call | tf_op jit(solution)/shard_map/pallas_call | solution.py:98
  10.7 1.2 reduce_sum.45
  12.2 81.4 %psum.7 = f32[7,7]{0,1:T(8,128)S(1)} all-reduce(f32[7,7]{0,1:T(8,128)S(1)} %multiply_add_fusion), channel_id=1, replica_groups=mesh['slab_0'=8,'slab_1'=4,'slab_2'=2,'pencil'=4] {'slab_0','slab_1','sl..., use_global_device_ids=true, to_apply=%region_3.4 | all-reduce | flops 49 | bytes 392 | tf_op jit(solution)/shard_map/psum | solution.py:157
  96.3 0.8 fusion.37
  97.0 1.2 broadcast_divide_fusion.weights_ref
  98.2 6.6 %shard_map.168 = f32[8,80,320]{2,1,0:T(8,128)} custom-call(f32[7]{0:T(128)} %broadcast_divide_fusion.weights_ref, f32[7,8,80,320]{3,2,1,0:T(8,128)} %field_ref.4), custom_call_target="tpu_custom_call" | custom-call | tf_op jit(solution)/shard_map/pallas_call | solution.py:128
  104.8 2.2 fusion.38
  107.6 1.5 all_to_all.32
  109.2 13.9 %all_to_all.39 = f32[4,1,51200]{2,1,0:T(1,128)S(1)} all-to-all(f32[4,1,51200]{2,1,0:T(1,128)S(1)} %all_to_all.32), channel_id=1, replica_groups=mesh['slab_0'=8,'slab_1'=4,'slab_2'=2,'pencil'=4] {'pencil'}, dimensions={0} | all-to-all | bytes 1638400 | tf_op jit(solution)/shard_map/all_to_all | solution.py:165
  123.0 2.4 reduce.8
  125.4 0.8 reshape.186
  126.2 1.2 convolution_bitcast_fusion.1
  127.5 8.9 %copy.56 = f32[320,80,8]{2,1,0:T(8,128)} copy(f32[320,80,8]{0,1,2:T(8,128)S(1)} %convolution_bitcast_fusion.1) | data formatting | bytes 1638400 | tf_op jit(solution)/shard_map/lqy,qkzy->lkz/dot_general | solution.py:167
  136.3 10.6 %all_to_all.33 = f32[64,1,3200]{2,1,0:T(1,128)} reshape(f32[320,80,8]{2,1,0:T(8,128)} %copy.56) | data formatting | bytes 1638400 | tf_op jit(solution)/shard_map/all_to_all | solution.py:168
  147.0 7.9 %all-to-all-start.1 = ((f32[64,1,3200]{2,1,0:T(1,128)}), f32[64,1,3200]{2,1,0:T(1,128)S(1)}, u32[]{:S(2)}, u32[]{:S(2)}) async-start(f32[64,1,3200]{2,1,0:T(1,128)} %all_to_all.33), calls=%async_computation.1 | async-start | bytes 1638400 | tf_op jit(solution)/shard_map/all_to_all | solution.py:168
  155.2 23.4 %all-to-all-done.1 = f32[64,1,3200]{2,1,0:T(1,128)S(1)} async-done(((f32[64,1,3200]{2,1,0:T(1,128)}), f32[64,1,3200]{2,1,0:T(1,128)S(1)}, u32[]{:S(2)}, u32[]{:S(2)}) %all-to-all-start.1) | async-done | bytes 819232 | tf_op jit(solution)/shard_map/all_to_all | solution.py:168
  178.6 1.5 copy.58
  180.1 2.4 fusion.16
  182.5 1.4 convolution_bitcast_fusion
  184.5 1.4 copy.61
  185.9 29.4 %all_to_all.40 = f32[64,1,3200]{2,1,0:T(1,128)S(1)} all-to-all(f32[64,1,3200]{2,1,0:T(1,128)S(1)} %copy.61), channel_id=1, replica_groups=mesh['slab_0'=8,'slab_1'=4,'slab_2'=2,'pencil'=4] {'slab_0','slab_1','sl..., dimensions={0} | all-to-all | bytes 1638400 | tf_op jit(solution)/shard_map/all_to_all | solution.py:177
  215.3 1.9 reduce.9
  217.2 8.9 %reshape.188 = f32[320,80,8]{2,1,0:T(8,128)} reshape(f32[64,3200]{1,0:T(8,128)S(1)} %reduce.9) | data formatting | bytes 1638400 | tf_op jit(solution)/shard_map/reshape | solution.py:178
  226.1 25.3 %fusion.4 = f32[4,80,8,80]{3,2,0,1:T(8,128)S(1)} fusion(f32[320,4,80,1]{0,2,1,3:T(8,128)S(1)} %copy-done.2, f32[320,80,8,1]{2,1,0,3:T(8,128)} %bitcast.57), kind=kOutput, calls=%fused_computation.6 | convolution fusion | flops 393216000 | bytes 2048000 | tf_op jit(solution)/shard_map/lqy,lkz->qkzy/dot_general | solution.py:179
  251.6 2.3 all_to_all.34
  253.9 3.7 %all-to-all-start.3 = ((f32[4,1,51200]{2,1,0:T(1,128)}), f32[4,1,51200]{2,1,0:T(1,128)S(1)}, u32[]{:S(2)}, u32[]{:S(2)}) async-start(f32[4,1,51200]{2,1,0:T(1,128)} %all_to_all.34), calls=%async_computation.3 | async-start | bytes 1638400 | tf_op jit(solution)/shard_map/all_to_all | solution.py:180
  258.4 10.9 %all-to-all-done.3 = f32[4,1,51200]{2,1,0:T(1,128)S(1)} async-done(((f32[4,1,51200]{2,1,0:T(1,128)}), f32[4,1,51200]{2,1,0:T(1,128)S(1)}, u32[]{:S(2)}, u32[]{:S(2)}) %all-to-all-start.3) | async-done | bytes 819232 | tf_op jit(solution)/shard_map/all_to_all | solution.py:180
  269.3 2.4 reduce.10
  271.7 0.8 reshape.189
  272.5 2.4 fusion.7.rest_0_
  274.8 6.6 %shard_map.169 = f32[8,80,320]{2,1,0:T(8,128)} custom-call(f32[7]{0:T(128)} %broadcast_divide_fusion.weights_ref, f32[7,8,80,320]{3,2,1,0:T(8,128)} %field_ref.5, f32[8,80,320]{2,1,0:T(8,128)} %fusion.7.rest_0_), custom_call_target="tpu_custom_call" | custom-call | tf_op jit(solution)/shard_map/pallas_call | solution.py:128
  (47 shorter events, 6.3 us)
Async XLA Ops:
  3.4 8.5 %copy-start.6 = (f32[49,28]{0,1:T(8,128)S(1)}, f32[49,28]{0,1:T(8,128)}, u32[]{:S(2)}) copy-start(f32[49,28]{0,1:T(8,128)} %constant.132.clone) | copy-start | bytes 16468
  98.2 6.6 %copy-start = (f32[320,320,1]{1,0,2:T(8,128)S(1)}, f32[320,320,1]{1,0,2:T(8,128)}, u32[]{:S(2)}) copy-start(f32[320,320,1]{1,0,2:T(8,128)} %constant.147) | copy-start | bytes 1228804
  123.0 3.2 %copy-start.1 = (f32[320,4,80,1]{0,2,1,3:T(8,128)S(1)}, f32[320,4,80,1]{0,2,1,3:T(8,128)}, u32[]{:S(2)}) copy-start(f32[320,4,80,1]{0,2,1,3:T(8,128)} %constant.146) | copy-start | bytes 1228804
  147.0 8.0 %copy-start.9 = (f32[320]{0:T(512)S(1)}, f32[320]{0:T(512)}, u32[]{:S(2)}) copy-start(f32[320]{0:T(512)} %constant.136.clone) | copy-start | bytes 3844
  147.0 8.1 %copy-start.8 = (f32[512]{0:T(512)S(1)}, f32[512]{0:T(512)}, u32[]{:S(2)}) copy-start(f32[512]{0:T(512)} %constant.144) | copy-start | bytes 6148
  147.0 31.6 %all-to-all-start.1 = ((f32[64,1,3200]{2,1,0:T(1,128)}), f32[64,1,3200]{2,1,0:T(1,128)S(1)}, u32[]{:S(2)}, u32[]{:S(2)}) async-start(f32[64,1,3200]{2,1,0:T(1,128)} %all_to_all.33), calls=%async_computation.1 | async-start | bytes 1638400 | tf_op jit(solution)/shard_map/all_to_all | solution.py:168
  180.1 2.4 copy-start.3
  217.2 8.9 %copy-start.2 = (f32[320,4,80,1]{0,2,1,3:T(8,128)S(1)}, f32[320,4,80,1]{0,2,1,3:T(8,128)}, u32[]{:S(2)}) copy-start(f32[320,4,80,1]{0,2,1,3:T(8,128)} %constant.146) | copy-start | bytes 1228804
  251.6 6.0 %copy-start.4 = (f32[7,24,324]{2,1,0:T(8,128)S(1)}, f32[7,24,324]{2,1,0:T(8,128)}, u32[]{:S(2)}) copy-start(f32[7,24,324]{2,1,0:T(8,128)} %param.19) | copy-start | bytes 653188
  251.6 6.0 %copy-start.5 = (f32[7,24,324]{2,1,0:T(8,128)S(1)}, f32[7,24,324]{2,1,0:T(8,128)}, u32[]{:S(2)}) copy-start(f32[7,24,324]{2,1,0:T(8,128)} %param.18) | copy-start | bytes 653188
  251.6 6.0 %copy-start.7 = (f32[7]{0:T(128)S(1)}, f32[7]{0:T(128)}, u32[]{:S(2)}) copy-start(f32[7]{0:T(128)} %broadcast_divide_fusion.weights_ref) | copy-start | bytes 88
  253.9 15.5 %all-to-all-start.3 = ((f32[4,1,51200]{2,1,0:T(1,128)}), f32[4,1,51200]{2,1,0:T(1,128)S(1)}, u32[]{:S(2)}, u32[]{:S(2)}) async-start(f32[4,1,51200]{2,1,0:T(1,128)} %all_to_all.34), calls=%async_computation.3 | async-start | bytes 1638400 | tf_op jit(solution)/shard_map/all_to_all | solution.py:180
where the time goes:
time: 283 us; the launch traced here: 281 us
  blocking collectives  125 us (44%)
  local copies, waits for them, and re-layouts  38.3 us (14%)
  matrix products  35.9 us (13%)
  waiting for transfers between devices  34.3 us (12%)
  Pallas kernels  20.5 us (7%)
  other arithmetic  14.7 us (5%)
  starting transfers between devices  11.7 us (4%)
    psum x1, blocking collectives, body(): weights = mixing_weights(lax.psum(grid_local + block_local, SLAB_PENCIL))  81.4 us
    all_to_all x1, blocking collectives, body(): lax.all_to_all(h.reshape(slabs, -1), SLAB, split_axis=0, concat_axis=0, t...  29.4 us
    dot_general x1, matrix products, body(): jnp.einsum('lqy,lkz->qkzy', qy.reshape(y_length, pencils, y_local), h, pr...  25.3 us
    all_to_all x1, waiting for transfers between devices, body(): lax.all_to_all(h.reshape(slabs, -1), SLAB, split_axis=0, concat_axis=0, t...  23.4 us
    all_to_all x1, blocking collectives, body(): h = lax.all_to_all(h, 'pencil', split_axis=0, concat_axis=0, tiled=True)  13.9 us
    all_to_all x3, local copies, waits for them, and re-layouts, body(): lax.all_to_all(h.reshape(slabs, -1), SLAB, split_axis=0, concat_axis=0, t...  13.5 us
    pallas_call x2, Pallas kernels, mix(): pl.pallas_call(functools.partial(mix_kernel, history), grid=(planes,), in...  13.2 us
    all_to_all x1, waiting for transfers between devices, body(): lax.all_to_all(h.reshape(pencils, -1), 'pencil', split_axis=0, concat_axi...  10.9 us
  transfers between devices with their start and end apart: 2, of which 2 were waited for; matrix products, arithmetic and copies ran while one was open for 0% of the time, Pallas kernels for 0%

commit v1 on v0

v1 whole, which is shorter than its diff:
```python
import functools
import math

import numpy as np

import jax
import jax.numpy as jnp
from jax import lax
from jax.experimental import pallas as pl
from jax.experimental.pallas import tpu as pltpu
from jax.sharding import Mesh
from jax.sharding import PartitionSpec as P

ORBITALS = 18
SLAB = ("slab_0", "slab_1", "slab_2")
SLAB_PENCIL = ("slab_0", "slab_1", "slab_2", "pencil")
MESH = pl.DeviceIdType.MESH

grid_mixing = 0.5
block_mixing = 0.5
kerker_wave = 6.0
species_orbitals = (18, 13, 8, 5)

H = 7
SLABS = 64
PENCILS = 4
ZL = 8
YL = 80
NX = 320
NY = YL * PENCILS
NZ = ZL * SLABS
KY = NY // SLABS
LT = 5
WIDE = 64
NARROW = 16
PAIRS = [(i, j) for i in range(H) for j in range(i + 1)]


def real_basis(length):
    half = length // 2
    n = np.arange(length)
    rows = [np.full(length, 1.0 / math.sqrt(length))]
    for k in range(1, half):
        angle = 2.0 * math.pi * ((k * n) % length) / length
        rows.append(math.sqrt(2.0 / length) * np.cos(angle))
        rows.append(math.sqrt(2.0 / length) * np.sin(angle))
    rows.append(np.where(n % 2 == 0, 1.0, -1.0) / math.sqrt(length))
    return np.stack(rows)


def two_parts(table):
    upper = table.astype(np.float32).astype(jnp.bfloat16)
    lower = (table - upper.astype(np.float64)).astype(np.float32).astype(jnp.bfloat16)
    return upper, lower


def block_mask(species, slot_count):
    live = jnp.arange(species.shape[0], dtype=jnp.int32) < slot_count[0]
    orbitals = jnp.zeros_like(species)
    for species_index, orbital_number in enumerate(species_orbitals):
        orbitals = orbitals + orbital_number * (species == species_index).astype(jnp.int32)
    entry = jnp.arange(ORBITALS * ORBITALS, dtype=jnp.int32)
    row_index = entry // ORBITALS
    column_index = entry % ORBITALS
    inside = (
        (row_index[None, :] < orbitals[:, None])
        & (column_index[None, :] < orbitals[:, None])
        & live[:, None]
    )
    return inside.astype(jnp.float32)


def split(value):
    upper = value.astype(jnp.bfloat16)
    lower = (value - upper.astype(jnp.float32)).astype(jnp.bfloat16)
    return upper, lower


def dot3(ah, al, bh, bl):
    dot = functools.partial(jnp.dot, preferred_element_type=jnp.float32)
    return dot(ah, bh) + (dot(ah, bl) + dot(al, bh))


def lanes_of(shape):
    return lax.broadcasted_iota(jnp.int32, shape, 1)


def swap(a, b):
    low = lanes_of(a.shape) < 64
    return (
        jnp.where(low, a, pltpu.roll(b, 64, 1)),
        jnp.where(low, pltpu.roll(a, 64, 1), b),
    )


def regroup(pieces, place):
    lane = lanes_of(pieces[0].shape)
    total = jnp.zeros_like(pieces[0])
    for n, piece in enumerate(pieces):
        shift = (16 * (n - place)) % 128
        moved = pltpu.roll(piece, shift, 1) if shift else piece
        total = jnp.where((lane >= 16 * n) & (lane < 16 * n + 16), moved, total)
    return total


def kernel(
    res, den, occ_h, occ_r, mask, t0, t1, t2, t3, t4, t5, t6, t7,
    out, occ_out,
    r7, d7, tx0, tx1, tx2, tx3, tz0, tz1, tz2, tz3,
    row_mine, row_pencil, row_group, row_slab, weight,
    mh, ml, hs, xs, yin, ys, zin, zh, zl, fac, zu, zout, yb, yo, xi, dm,
    load_sem, table_sem, send_sem, recv_sem,
):
    s0, s1, s2 = (lax.axis_index(a) for a in SLAB)
    me_p = lax.axis_index("pencil")
    me_s = (s0 * 4 + s1) * 2 + s2

    def slab_at(r):
        t = lax.rem(me_s + r, SLABS)
        return t, (t // 8, lax.rem(t // 2, 4), lax.rem(t, 2), me_p)

    def pencil_at(r):
        q = lax.rem(me_p + r, PENCILS)
        return q, (s0, s1, s2, q)

    loads = []
    for z in range(ZL):
        rows = pl.ds(z * YL, YL)
        loads.append(pltpu.make_async_copy(res.at[:, rows], r7.at[:, rows], load_sem.at[z]))
    for c in loads:
        c.start()
    tables = []
    for n, (a, b) in enumerate(
        zip((t0, t1, t2, t3, t4, t5, t6, t7), (tx0, tx1, tx2, tx3, tz0, tz1, tz2, tz3))
    ):
        tables.append(pltpu.make_async_copy(a, b, table_sem.at[n]))
    tables.append(pltpu.make_async_copy(den, d7, table_sem.at[8]))

    barrier = pltpu.get_barrier_semaphore()
    for r in range(1, PENCILS):
        pl.semaphore_signal(barrier, inc=1, device_id=pencil_at(r)[1], device_id_type=MESH)

    def greet(r, c):
        pl.semaphore_signal(barrier, inc=1, device_id=slab_at(r)[1], device_id_type=MESH)
        return c

    lax.fori_loop(1, SLABS, greet, 0)

    zero = jnp.zeros((8, 128), jnp.float32)

    def add_products(acc, v):
        return [acc[n] + v[i] * v[j] for n, (i, j) in enumerate(PAIRS)]

    def pad(v):
        return jnp.concatenate([v, jnp.zeros((8, 128 - v.shape[1]), v.dtype)], axis=1)

    def block_step(r, acc):
        at = pl.ds(pl.multiple_of(r * 8, 8), 8)
        acc = list(acc)
        for lo, hi in ((0, 128), (128, 256), (256, 324)):
            m = mask[at, lo:hi]
            v = [occ_r[i, at, lo:hi] * m for i in range(H)]
            acc = add_products(acc, v if hi - lo == 128 else [pad(x) for x in v])
        return tuple(acc)

    block = lax.fori_loop(0, 3, block_step, (zero,) * len(PAIRS))
    cells = NX * NY * NZ
    scale = cells / (100.0 * SLABS * PENCILS * mask.shape[0])
    acc = tuple(x * scale for x in block)

    def grid_step(r, acc):
        at = pl.ds(pl.multiple_of(r * 8, 8), 8)
        acc = list(acc)
        for lo, hi in ((0, 128), (128, 256), (256, 320)):
            v = [r7[i, at, lo:hi] for i in range(H)]
            acc = add_products(acc, v if hi - lo == 128 else [pad(x) for x in v])
        return tuple(acc)

    for z in range(ZL):
        loads[z].wait()
        acc = lax.fori_loop(z * 10, z * 10 + 10, grid_step, acc)
    for c in tables:
        c.start()

    lane = lanes_of((8, 128))
    sub = lax.broadcasted_iota(jnp.int32, (8, 128), 0)
    spread = zero
    for n0 in range(0, len(PAIRS), 8):
        tile = zero
        for r, x in enumerate(acc[n0 : n0 + 8]):
            tile = jnp.where(sub == r, jnp.sum(x, axis=0, keepdims=True), tile)
        column = jnp.sum(tile, axis=1, keepdims=True)
        for r, (i, j) in enumerate(PAIRS[n0 : n0 + 8]):
            here = (sub == r) & ((lane == 8 * i + j) | (lane == 8 * j + i))
            spread = jnp.where(here, column, spread)
    row_mine[0] = jnp.sum(spread, axis=0, keepdims=True)

    pl.semaphore_wait(barrier, PENCILS - 1 + SLABS - 1)

    def exchange(phase, source_at, target, me, at, count, unroll):
        def copy(r):
            q, device = at(r)
            return pltpu.make_async_remote_copy(
                src_ref=source_at(q),
                dst_ref=target(me),
                send_sem=send_sem.at[phase],
                recv_sem=recv_sem.at[phase],
                device_id=device,
                device_id_type=MESH,
            )

        if unroll:
            for r in range(1, count):
                copy(r).start()
        else:
            lax.fori_loop(1, count, lambda r, c: (copy(r).start(), c)[1], 0)
        pltpu.make_async_copy(source_at(me), target(me), recv_sem.at[phase]).start()

        def finish():
            if unroll:
                for r in range(1, count):
                    copy(r).wait_send()
            else:
                lax.fori_loop(1, count, lambda r, c: (copy(r).wait_send(), c)[1], 0)

        return finish

    def arrive(phase, whole):
        pltpu.make_async_copy(whole, whole, recv_sem.at[phase]).wait()

    done = []
    done.append(
        exchange(
            0, lambda q: row_mine.at[0], lambda m: row_pencil.at[m], me_p, pencil_at, PENCILS, True
        )
    )
    arrive(0, row_pencil)
    row_group[0] = (row_pencil[0] + row_pencil[1]) + (row_pencil[2] + row_pencil[3])
    done.append(
        exchange(
            1, lambda q: row_group.at[0], lambda m: row_slab.at[m], me_s, slab_at, SLABS, False
        )
    )
    arrive(1, row_slab)
    total = row_slab.reshape(SLABS, 128)[...]
    total = jnp.sum(total, axis=0, keepdims=True) * (1.0 / cells)

    m = zero
    for i in range(H):
        m = jnp.where(sub == i, pltpu.roll(total, (128 - 8 * i) % 128, 1) if i else total, m)
    m = jnp.where(lane < H, m, 0.0)
    m = jnp.where((lane == H) & (sub < H), 1.0, m)
    for k in range(H):
        pivot_row = m[k : k + 1, :] / m[k : k + 1, k : k + 1]
        m = jnp.where(sub == k, pivot_row, m - m[:, k : k + 1] * pivot_row)
    solved = m[:, H : H + 1]
    weight[...] = jnp.broadcast_to(solved / jnp.sum(solved, axis=0, keepdims=True), (8, 128))

    w320 = [
        jnp.broadcast_to(weight[i : i + 1, 0:1], (16, NX)) for i in range(H)
    ]

    def mix_step(r, c):
        at = pl.ds(pl.multiple_of(r * 16, 16), 16)
        v = w320[0] * r7[0, at]
        for i in range(1, H):
            v += w320[i] * r7[i, at]
        mh[at, :], ml[at, :] = split(v)
        return c

    lax.fori_loop(0, ZL * YL // 16, mix_step, 0)
    for c in tables[:4]:
        c.wait()

    def x_step(j, c):
        at = pl.ds(pl.multiple_of(j * 160, 160), 160)
        h = dot3(mh[at, :], ml[at, :], tx2[...], tx3[...])
        hs[at, 0:256] = h[:, 0:256]
        hs[at, 256:384] = jnp.concatenate(
            [h[:, 256:320], jnp.zeros((160, 64), jnp.float32)], axis=1
        )
        return c

    lax.fori_loop(0, 4, x_step, 0)
    for j in range(4):
        for c in range(2):
            a = hs[2 * j * YL : (2 * j + 1) * YL, 128 * c : 128 * c + 128]
            b = hs[(2 * j + 1) * YL : (2 * j + 2) * YL, 128 * c : 128 * c + 128]
            xs[2 * c, j], xs[2 * c + 1, j] = swap(a, b)
    for b in range(PENCILS):
        xs[b, 4] = regroup([hs[z * YL : (z + 1) * YL, 256:384] for z in range(ZL)], b)
    done.append(
        exchange(2, lambda q: xs.at[q], lambda m: yin.at[m], me_p, pencil_at, PENCILS, True)
    )

    def factor_step(r, c):
        at = pl.ds(pl.multiple_of(r * 8, 8), 8)
        kz = (lax.broadcasted_iota(jnp.int32, (8, 512), 0) + r * 8 + 1) // 2
        line = lanes_of((8, 512))
        wide = line < 384
        within = line - 384
        kx = jnp.where(wide, me_p * WIDE + lax.rem(line, 64), 256 + me_p * NARROW + lax.rem(within, 16))
        ky = me_s * KY + jnp.where(wide, line // 64, within // 16)
        kx = (kx + 1) // 2
        ky = (ky + 1) // 2
        square = (kz * kz + ky * ky + kx * kx).astype(jnp.float32)
        fac[at, :] = square / (square + kerker_wave * kerker_wave)
        return c

    lax.fori_loop(0, NZ // 8, factor_step, 0)

    for lo, hi in ((0, 128), (128, 256), (256, 324)):
        v = jnp.zeros((24, hi - lo), jnp.float32)
        for i in range(H):
            w = jnp.broadcast_to(weight[i : i + 1, 0:1], (24, hi - lo))
            v += w * (occ_h[i, :, lo:hi] + block_mixing * occ_r[i, :, lo:hi])
        occ_out[:, lo:hi] = mask[:, lo:hi] * v

    arrive(2, yin)

    y = jnp.concatenate([yin[:, n].reshape(NY, 128) for n in range(LT)], axis=1)
    yh, yl = split(y)
    y = dot3(tx0[...], tx1[...], yh, yl)
    for n in range(LT):
        ys[n] = y[:, 128 * n : 128 * n + 128]
    ys_rows = ys.reshape(LT, NY, 1, 128)
    zin_rows = zin.reshape(LT, KY, SLABS, 1, 128)
    done.append(
        exchange(
            3,
            lambda q: ys_rows.at[:, pl.ds(q * KY, KY)],
            lambda m: zin_rows.at[:, :, m],
            me_s, slab_at, SLABS, False,
        )
    )

    for c in tables[4:]:
        c.wait()

    def density_step(r, c):
        at = pl.ds(pl.multiple_of(r * 16, 16), 16)
        v = w320[0] * d7[0, at]
        for i in range(1, H):
            v += w320[i] * d7[i, at]
        dm[at, :] = v
        return c

    lax.fori_loop(0, ZL * YL // 16, density_step, 0)
    arrive(3, zin)

    def put(z, tile, value):
        at = slice(64 * z, 64 * z + 64)
        lanes = slice(128 * tile, 128 * tile + 128)
        zh[at, lanes], zl[at, lanes] = split(value)

    for j in range(4):
        for tile, ky in ((0, 0), (1, 2), (2, 4)):
            a, b = swap(zin[j, ky], zin[j, min(ky + 1, 4)])
            put(2 * j, tile, a)
            put(2 * j + 1, tile, b)
    for z in range(ZL):
        put(z, 3, regroup([zin[4, ky] for ky in range(KY)], z))
    for n in range(2):
        lanes = slice(256 * n, 256 * n + 256)
        u = dot3(tz0[...], tz1[...], zh[:, lanes], zl[:, lanes])
        zu[:, lanes] = u * fac[:, lanes]
    for r in range(8):
        at = slice(64 * r, 64 * r + 64)
        zh[at, :], zl[at, :] = split(zu[at, :])
    for n in range(2):
        lanes = slice(256 * n, 256 * n + 256)
        zu[:, lanes] = dot3(tz2[...], tz3[...], zh[:, lanes], zl[:, lanes])

    def got(z, tile):
        return zu[64 * z : 64 * z + 64, 128 * tile : 128 * tile + 128]

    for j in range(4):
        for tile, ky in ((0, 0), (1, 2), (2, 4)):
            a, b = swap(got(2 * j, tile), got(2 * j + 1, tile))
            zout[j, ky] = a
            if ky < 4:
                zout[j, ky + 1] = b
    for ky in range(KY):
        zout[4, ky] = regroup([got(z, 3) for z in range(ZL)], ky)
    zout_rows = zout.reshape(LT, KY, SLABS, 1, 128)
    yb_rows = yb.reshape(LT, NY, 1, 128)
    done.append(
        exchange(
            4,
            lambda q: zout_rows.at[:, :, q],
            lambda m: yb_rows.at[:, pl.ds(m * KY, KY)],
            me_s, slab_at, SLABS, False,
        )
    )
    arrive(4, yb)

    y = jnp.concatenate([yb[n] for n in range(LT)], axis=1)
    yh, yl = split(y)
    y = dot3(tx2[...], tx3[...], yh, yl)
    for n in range(LT):
        yo[:, n] = y[:, 128 * n : 128 * n + 128].reshape(PENCILS, YL, 128)
    done.append(
        exchange(5, lambda q: yo.at[q], lambda m: xi.at[m], me_p, pencil_at, PENCILS, True)
    )
    arrive(5, xi)

    for j in range(4):
        for c in range(2):
            a, b = swap(xi[2 * c, j], xi[2 * c + 1, j])
            hs[2 * j * YL : (2 * j + 1) * YL, 128 * c : 128 * c + 128] = a
            hs[(2 * j + 1) * YL : (2 * j + 2) * YL, 128 * c : 128 * c + 128] = b
    for z in range(ZL):
        hs[z * YL : (z + 1) * YL, 256:384] = regroup([xi[b, 4] for b in range(PENCILS)], z)

    def end_step(j, c):
        at = pl.ds(pl.multiple_of(j * 160, 160), 160)
        h = jnp.concatenate([hs[at, 0:256], hs[at, 256:384][:, :64]], axis=1)
        vh, vl = split(h)
        out[at, :] = dm[at, :] + grid_mixing * dot3(vh, vl, tx0[...], tx1[...])
        return c

    lax.fori_loop(0, 4, end_step, 0)
    for finish in done:
        finish()


def body(
    density_history, residual_history, occupancy_history, occupancy_residual, species, slot_count
):
    mask = block_mask(species, slot_count)
    qx = real_basis(NX)
    qz = real_basis(NZ)
    qz = qz.reshape(NZ, SLABS, ZL).transpose(0, 2, 1).reshape(NZ, NZ)
    tables = two_parts(qx) + two_parts(qx.T) + two_parts(qz) + two_parts(qz.T)
    f32 = jnp.float32
    bf16 = jnp.bfloat16
    vmem = pl.BlockSpec(memory_space=pltpu.VMEM)
    hbm = pl.BlockSpec(memory_space=pl.ANY)
    rows = ZL * YL
    new_density, new_occupancy = pl.pallas_call(
        kernel,
        in_specs=[hbm, hbm, vmem, vmem, vmem] + [hbm] * 8,
        out_specs=[vmem, vmem],
        out_shape=[
            jax.ShapeDtypeStruct((rows, NX), f32),
            jax.ShapeDtypeStruct(mask.shape, f32),
        ],
        scratch_shapes=[
            pltpu.VMEM((H, rows, NX), f32),
            pltpu.VMEM((H, rows, NX), f32),
        ]
        + [pltpu.VMEM((NX, NX), bf16)] * 4
        + [pltpu.VMEM((NZ, NZ), bf16)] * 4
        + [
            pltpu.VMEM((1, 1, 128), f32),
            pltpu.VMEM((PENCILS, 1, 128), f32),
            pltpu.VMEM((1, 1, 128), f32),
            pltpu.VMEM((SLABS, 1, 128), f32),
            pltpu.VMEM((8, 128), f32),
            pltpu.VMEM((rows, NX), bf16),
            pltpu.VMEM((rows, NX), bf16),
            pltpu.VMEM((rows, 384), f32),
            pltpu.VMEM((PENCILS, LT, YL, 128), f32),
            pltpu.VMEM((PENCILS, LT, YL, 128), f32),
            pltpu.VMEM((LT, NY, 128), f32),
            pltpu.VMEM((LT, KY, SLABS, 128), f32),
            pltpu.VMEM((NZ, 512), bf16),
            pltpu.VMEM((NZ, 512), bf16),
            pltpu.VMEM((NZ, 512), f32),
            pltpu.VMEM((NZ, 512), f32),
            pltpu.VMEM((LT, KY, SLABS, 128), f32),
            pltpu.VMEM((LT, NY, 128), f32),
            pltpu.VMEM((PENCILS, LT, YL, 128), f32),
            pltpu.VMEM((PENCILS, LT, YL, 128), f32),
            pltpu.VMEM((rows, NX), f32),
            pltpu.SemaphoreType.DMA((ZL,)),
            pltpu.SemaphoreType.DMA((9,)),
            pltpu.SemaphoreType.DMA((6,)),
            pltpu.SemaphoreType.DMA((6,)),
        ],
        compiler_params=pltpu.CompilerParams(
            collective_id=0, has_side_effects=True, vmem_limit_bytes=56 * 2**20
        ),
    )(
        residual_history.reshape(H, rows, NX),
        density_history.reshape(H, rows, NX),
        occupancy_history,
        occupancy_residual,
        mask,
        *tables,
    )
    return (new_density.reshape(ZL, YL, NX), new_occupancy)


def solution(mesh):
    torus = Mesh(
        mesh.devices.reshape(8, 4, 2, mesh.shape["pencil"]),
        ("slab_0", "slab_1", "slab_2", "pencil"),
    )
    placed = (
        P(None, SLAB, "pencil", None),
        P(None, SLAB, "pencil", None),
        P(None, SLAB_PENCIL, None),
        P(None, SLAB_PENCIL, None),
        P(SLAB_PENCIL),
        P(SLAB_PENCIL),
    )
    return jax.shard_map(
        body,
        mesh=torus,
        in_specs=placed,
        out_specs=(P(SLAB, "pencil", None), P(SLAB_PENCIL, None)),
        check_vma=False,
    )
```

time: 283 us -> 106 us (0.37)
  blocking collectives: 125 us -> 0 us
  Pallas kernels: 20.5 us -> 99.3 us
  matrix products: 35.9 us -> 0 us
  local copies, waits for them, and re-layouts: 38.3 us -> 3.6 us
  waiting for transfers between devices: 34.3 us -> 0 us
  other arithmetic: 14.7 us -> 1.37 us
  starting transfers between devices: 11.7 us -> 0 us
    psum x1 -> x0, blocking collectives: 81.4 us -> none  [body(): weights = mixing_weights(lax.psum(grid_local + block_local, SLAB_PENCIL))]
    pallas_call x3 -> x1, Pallas kernels: 20.5 us -> 99.3 us  [body(): pl.pallas_call(kernel, in_specs=[hbm, hbm, vmem, vmem, vmem] + [hbm] * 8,...]
    all_to_all x2 -> x0, blocking collectives: 43.3 us -> none  [the longest x1 29.4 us: body(): lax.all_to_all(h.reshape(slabs, -1), SLAB, split_axis=0, concat_axis=0, t...]
    dot_general x6 -> x0, matrix products: 35 us -> none  [the longest x1 25.3 us: body(): jnp.einsum('lqy,lkz->qkzy', qy.reshape(y_length, pencils, y_local), h, pr...]
    all_to_all x2 -> x0, waiting for transfers between devices: 34.3 us -> none  [the longest x1 23.4 us: body(): lax.all_to_all(h.reshape(slabs, -1), SLAB, split_axis=0, concat_axis=0, t...]
    all_to_all x5 -> x0, local copies, waits for them, and re-layouts: 17.3 us -> none  [the longest x3 13.5 us: body(): lax.all_to_all(h.reshape(slabs, -1), SLAB, split_axis=0, concat_axis=0, t...]
    all_to_all x2 -> x0, starting transfers between devices: 11.7 us -> none  [the longest x1 7.94 us: body(): lax.all_to_all(h.reshape(slabs, -1), SLAB, split_axis=0, concat_axis=0, t...]
    reshape x3 -> x0, local copies, waits for them, and re-layouts: 10.4 us -> none  [the longest x1 8.87 us: body(): h = h.reshape(y_length, kx_local, z_local)]
  transfers between devices with their start and end apart: 2 -> 0, of which waited for: 2 -> 0; matrix products, arithmetic and copies ran while one was open for 0% -> 0% of each run, Pallas kernels for 0% -> 0%
where the time goes in v1:
time: 106 us
  Pallas kernels  99.3 us (94%)
  local copies, waits for them, and re-layouts  3.6 us (3%)
  other arithmetic  1.37 us (1%)
  between operations  1.29 us (1%)
    pallas_call x1, Pallas kernels, body(): pl.pallas_call(kernel, in_specs=[hbm, hbm, vmem, vmem, vmem] + [hbm] * 8,...  99.3 us
    unnamed x2, local copies, waits for them, and re-layouts  3.6 us

profile of v1, /device:TPU:1, one launch (start us, length us, event | category | flops | bytes accessed | tf_op | source)
XLA Modules:
  0.0 105.6 jit_solution(12826678772641629102)
XLA Ops:
  1.3 0.7 fusion.9
  2.0 0.7 and_convert_fusion.mask
  2.7 99.3 %shard_map.149 = (f32[640,320]{1,0:T(8,128)}, f32[24,324]{1,0:T(8,128)}) custom-call(f32[7,640,320]{2,1,0:T(8,128)} %bitcast.5, f32[7,640,320]{2,1,0:T(8,128)} %bitcast.6, f32[7,24,324]{2,1,0:T(8,128)} %occ_h.1, f32[7,24,324]{2,1,0:T(8,128)} %occ_r.1, f32[24,324]{1,0:T(8,128)} %and_convert_fusion.mask, bf16[320,320]{1,0:T(8,128)(2,1)} %constant.53.clone.t0, ...), custom_call_target="tpu_custom_call" | custom-call | tf_op jit(solution)/shard_map/pallas_call | solution.py:440
  102.0 2.2 %copy.19 = f32[8,80,320]{2,1,0:T(8,128)} copy(f32[8,80,320]{2,1,0:T(8,128)} %bitcast.7) | data formatting | bytes 1638400
  104.2 1.4 %copy.20 = f32[24,324]{1,0:T(8,128)} copy(f32[24,324]{1,0:T(8,128)} %get-tuple-element.11) | data formatting | bytes 62208
  (2 shorter events, 0.0 us)

commit v2 on v1

v2 whole, which is shorter than its diff:
```python
import functools
import math

import numpy as np

import jax
import jax.numpy as jnp
from jax import lax
from jax.experimental import pallas as pl
from jax.experimental.pallas import tpu as pltpu
from jax.sharding import Mesh
from jax.sharding import PartitionSpec as P

ORBITALS = 18
SLAB = ("slab_0", "slab_1", "slab_2")
SLAB_PENCIL = ("slab_0", "slab_1", "slab_2", "pencil")
MESH = pl.DeviceIdType.MESH

grid_mixing = 0.5
block_mixing = 0.5
kerker_wave = 6.0
species_orbitals = (18, 13, 8, 5)

H = 7
SLABS = 64
PENCILS = 4
ZL = 8
YL = 80
NX = 320
NY = YL * PENCILS
NZ = ZL * SLABS
KY = NY // SLABS
LT = 5
CHUNKS = ((0,), (1, 2), (3, 4))
EIGHT = 8
PAIRS = [(i, j) for i in range(H) for j in range(i + 1)]


def real_basis(length):
    half = length // 2
    n = np.arange(length)
    rows = [np.full(length, 1.0 / math.sqrt(length))]
    for k in range(1, half):
        angle = 2.0 * math.pi * ((k * n) % length) / length
        rows.append(math.sqrt(2.0 / length) * np.cos(angle))
        rows.append(math.sqrt(2.0 / length) * np.sin(angle))
    rows.append(np.where(n % 2 == 0, 1.0, -1.0) / math.sqrt(length))
    return np.stack(rows)


def two_parts(table):
    upper = table.astype(np.float32).astype(jnp.bfloat16)
    lower = (table - upper.astype(np.float64)).astype(np.float32).astype(jnp.bfloat16)
    return upper, lower


def block_mask(species, slot_count):
    live = jnp.arange(species.shape[0], dtype=jnp.int32) < slot_count[0]
    orbitals = jnp.zeros_like(species)
    for species_index, orbital_number in enumerate(species_orbitals):
        orbitals = orbitals + orbital_number * (species == species_index).astype(jnp.int32)
    entry = jnp.arange(ORBITALS * ORBITALS, dtype=jnp.int32)
    row_index = entry // ORBITALS
    column_index = entry % ORBITALS
    inside = (
        (row_index[None, :] < orbitals[:, None])
        & (column_index[None, :] < orbitals[:, None])
        & live[:, None]
    )
    return inside.astype(jnp.float32)


def split(value):
    upper = value.astype(jnp.bfloat16)
    lower = (value - upper.astype(jnp.float32)).astype(jnp.bfloat16)
    return upper, lower


def dot3(ah, al, bh, bl):
    dot = functools.partial(jnp.dot, preferred_element_type=jnp.float32)
    return dot(ah, bh) + (dot(ah, bl) + dot(al, bh))


def lanes_of(shape):
    return lax.broadcasted_iota(jnp.int32, shape, 1)


def regroup(pieces, place):
    lane = lanes_of(pieces[0].shape)
    total = jnp.zeros_like(pieces[0])
    for n, piece in enumerate(pieces):
        moved = pltpu.roll(piece, lax.rem(16 * (n - place) + 128, 128), 1)
        total = jnp.where((lane >= 16 * n) & (lane < 16 * n + 16), moved, total)
    return total


def repeat(count, step):
    lax.fori_loop(0, count, lambda i, c: (step(i), c)[1], 0)


def kernel(
    res, den, occ_h, occ_r, mask, t0, t1, t2, t3, t4, t5, t6, t7,
    out, occ_out,
    r7, d7, tx0, tx1, tx2, tx3, tz0, tz1, tz2, tz3,
    row_mine, row_pencil, row_group, row_slab, weight,
    mh, ml, hs, xs, yin, ys, zin, zh, zl, fac, zu, zout, yb, yo, xi, dm,
    load_sem, table_sem, send_sem, recv_sem,
):
    s0, s1, s2 = (lax.axis_index(a) for a in SLAB)
    me_p = lax.axis_index("pencil")
    me_s = (s0 * 4 + s1) * 2 + s2

    def slab_each(act, cores=2):
        near = []
        for d in range(4 * cores):
            y, core = lax.rem(s1 + d // cores, 4), s2 if d % cores == 0 else 1 - s2
            near.append((y * cores + (core if cores == 2 else 0), y, core))

        def plane(z, some):
            for k, y, core in some:
                act(z * (4 * cores) + k, (z, y, core, me_p))

        plane(lax.rem(s0 + 4, 8), near)

        def pair(i):
            plane(lax.rem(s0 + 3 - i, 8), near)
            plane(lax.rem(s0 + 5 + i, 8), near)

        repeat(3, pair)
        plane(s0, near[1:])

    def pencil_each(act):
        for r in (2, 1, 3):
            q = lax.rem(me_p + r, PENCILS)
            act(q, (s0, s1, s2, q))

    me_e = s2 * PENCILS + me_p
    me_c = s0 * 4 + s1

    def eight_each(act):
        for r in range(1, EIGHT):
            q = lax.rem(me_p + r, PENCILS)
            core = s2 if r < PENCILS else 1 - s2
            act(core * PENCILS + q, (s0, s1, core, q))

    loads = []
    for z in range(ZL):
        rows = pl.ds(z * YL, YL)
        loads.append(pltpu.make_async_copy(res.at[:, rows], r7.at[:, rows], load_sem.at[z]))
    for c in loads:
        c.start()
    tables = []
    for n, (a, b) in enumerate(
        zip((t0, t1, t2, t3, t4, t5, t6, t7), (tx0, tx1, tx2, tx3, tz0, tz1, tz2, tz3))
    ):
        tables.append(pltpu.make_async_copy(a, b, table_sem.at[n]))
    tables.append(pltpu.make_async_copy(den, d7, table_sem.at[8]))

    barrier = pltpu.get_barrier_semaphore()
    def greet(q, device):
        pl.semaphore_signal(barrier, inc=1, device_id=device, device_id_type=MESH)

    eight_each(greet)
    slab_each(greet)

    zero = jnp.zeros((8, 128), jnp.float32)

    def add_products(acc, v):
        return [acc[n] + v[i] * v[j] for n, (i, j) in enumerate(PAIRS)]

    def pad(v):
        return jnp.concatenate([v, jnp.zeros((8, 128 - v.shape[1]), v.dtype)], axis=1)

    def block_step(r, acc):
        at = pl.ds(pl.multiple_of(r * 8, 8), 8)
        acc = list(acc)
        for lo, hi in ((0, 128), (128, 256), (256, 324)):
            m = mask[at, lo:hi]
            v = [occ_r[i, at, lo:hi] * m for i in range(H)]
            acc = add_products(acc, v if hi - lo == 128 else [pad(x) for x in v])
        return tuple(acc)

    block = lax.fori_loop(0, 3, block_step, (zero,) * len(PAIRS))
    cells = NX * NY * NZ
    scale = cells / (100.0 * SLABS * PENCILS * mask.shape[0])
    acc = tuple(x * scale for x in block)

    def grid_step(r, acc):
        at = pl.ds(pl.multiple_of(r * 8, 8), 8)
        acc = list(acc)
        for lo, hi in ((0, 128), (128, 256), (256, 320)):
            v = [r7[i, at, lo:hi] for i in range(H)]
            acc = add_products(acc, v if hi - lo == 128 else [pad(x) for x in v])
        return tuple(acc)

    for z in range(ZL):
        loads[z].wait()
        acc = lax.fori_loop(z * 10, z * 10 + 10, grid_step, acc)
    for c in tables:
        c.start()

    lane = lanes_of((8, 128))
    sub = lax.broadcasted_iota(jnp.int32, (8, 128), 0)
    spread = zero
    for n0 in range(0, len(PAIRS), 8):
        tile = zero
        for r, x in enumerate(acc[n0 : n0 + 8]):
            tile = jnp.where(sub == r, jnp.sum(x, axis=0, keepdims=True), tile)
        column = jnp.sum(tile, axis=1, keepdims=True)
        for r, (i, j) in enumerate(PAIRS[n0 : n0 + 8]):
            here = (sub == r) & ((lane == 8 * i + j) | (lane == 8 * j + i))
            spread = jnp.where(here, column, spread)
    row_mine[0] = jnp.sum(spread, axis=0, keepdims=True)

    pl.semaphore_wait(barrier, EIGHT - 1 + SLABS - 1)

    def exchange(phase, source_at, target, me, each, sent):
        def start(q, device):
            pltpu.make_async_remote_copy(
                src_ref=source_at(q),
                dst_ref=target(me),
                send_sem=send_sem.at[phase],
                recv_sem=recv_sem.at[phase],
                device_id=device,
                device_id_type=MESH,
            ).start()

        each(start)
        pltpu.make_async_copy(source_at(me), target(me), recv_sem.at[phase]).start()
        return pltpu.make_async_copy(sent, sent, send_sem.at[phase]).wait

    def arrive(phase, whole):
        pltpu.make_async_copy(whole, whole, recv_sem.at[phase]).wait()

    done = []
    done.append(
        exchange(
            0, lambda q: row_mine.at[0], lambda m: row_pencil.at[m], me_e, eight_each,
            row_pencil.at[pl.ds(0, EIGHT - 1)],
        )
    )
    arrive(0, row_pencil)
    group = row_pencil.reshape(EIGHT, 128)[...]
    row_group[0] = jnp.sum(group, axis=0, keepdims=True)
    done.append(
        exchange(
            1, lambda q: row_group.at[0], lambda m: row_slab.at[m], me_c,
            lambda act: slab_each(act, 1), row_slab.at[pl.ds(0, SLABS // 2 - 1)],
        )
    )

    def factor_step(r):
        at = pl.ds(pl.multiple_of(r * 8, 8), 8)
        kz = (lax.broadcasted_iota(jnp.int32, (8, 128), 0) + r * 8 + 1) // 2
        ky = (me_s * KY + lane // 16 + 1) // 2
        for g in range(LT):
            kx = (64 * g + 16 * me_p + lax.rem(lane, 16) + 1) // 2
            square = (kz * kz + ky * ky + kx * kx).astype(jnp.float32)
            fac[at, 128 * g : 128 * g + 128] = square / (square + kerker_wave * kerker_wave)

    repeat(NZ // 8, factor_step)

    arrive(1, row_slab)
    total = row_slab.reshape(SLABS // 2, 128)[...]
    total = jnp.sum(total, axis=0, keepdims=True) * (1.0 / cells)

    m = zero
    for i in range(H):
        m = jnp.where(sub == i, pltpu.roll(total, (128 - 8 * i) % 128, 1) if i else total, m)
    m = jnp.where(lane < H, m, 0.0)
    m = jnp.where((lane == H) & (sub < H), 1.0, m)
    for k in range(H):
        pivot_row = m[k : k + 1, :] / m[k : k + 1, k : k + 1]
        m = jnp.where(sub == k, pivot_row, m - m[:, k : k + 1] * pivot_row)
    solved = m[:, H : H + 1]
    weight[...] = jnp.broadcast_to(solved / jnp.sum(solved, axis=0, keepdims=True), (8, 128))

    w320 = [jnp.broadcast_to(weight[i : i + 1, 0:1], (16, NX)) for i in range(H)]

    def mix_step(r):
        at = pl.ds(pl.multiple_of(r * 16, 16), 16)
        v = w320[0] * r7[0, at]
        for i in range(1, H):
            v += w320[i] * r7[i, at]
        mh[at, :], ml[at, :] = split(v)

    repeat(ZL * YL // 16, mix_step)
    for c in tables[:4]:
        c.wait()

    def phase(c, stage):
        return 2 + 4 * c + stage

    for c, chunk in enumerate(CHUNKS):
        g0, g1 = chunk[0], chunk[-1] + 1
        n = g1 - g0
        tile = slice(128 * c, 128 * c + 128)

        def x_step(j):
            at = pl.ds(pl.multiple_of(j * 160, 160), 160)
            columns = slice(64 * g0, 64 * g1)
            h = dot3(mh[at, :], ml[at, :], tx2[:, columns], tx3[:, columns])
            if n == 1:
                h = jnp.concatenate([h, jnp.zeros((160, 64), jnp.float32)], axis=1)
            hs[at, tile] = h

        repeat(4, x_step)

        def x_pack(b):
            planes = [hs[z * YL : (z + 1) * YL, tile] for z in range(ZL)]
            for g in chunk:
                xs[b, g] = regroup(planes, 4 * (g - g0) + b)

        repeat(PENCILS, x_pack)
        done.append(
            exchange(
                phase(c, 0),
                lambda q, g0=g0, n=n: xs.at[q, pl.ds(g0, n)],
                lambda m, g0=g0, n=n: yin.at[m, pl.ds(g0, n)],
                me_p, pencil_each, xs.at[pl.ds(0, PENCILS - 1), pl.ds(g0, n)],
            )
        )

    for c in tables[4:]:
        c.wait()

    def density_step(r):
        at = pl.ds(pl.multiple_of(r * 16, 16), 16)
        v = w320[0] * d7[0, at]
        for i in range(1, H):
            v += w320[i] * d7[i, at]
        dm[at, :] = v

    ys_rows = ys.reshape(LT, NY, 1, 128)
    zin_rows = zin.reshape(LT, KY, SLABS, 1, 128)
    zout_rows = zout.reshape(LT, KY, SLABS, 1, 128)
    yb_rows = yb.reshape(LT, NY, 1, 128)
    for c, chunk in enumerate(CHUNKS):
        g0, n = chunk[0], len(chunk)
        arrive(phase(c, 0), yin.at[:, pl.ds(g0, n)])
        y = jnp.concatenate([yin[:, g].reshape(NY, 128) for g in chunk], axis=1)
        y = dot3(tx0[...], tx1[...], *split(y))
        for g in chunk:
            ys[g] = y[:, 128 * (g - g0) : 128 * (g - g0) + 128]
        done.append(
            exchange(
                phase(c, 1),
                lambda q, g0=g0, n=n: ys_rows.at[pl.ds(g0, n), pl.ds(q * KY, KY)],
                lambda m, g0=g0, n=n: zin_rows.at[pl.ds(g0, n), :, m],
                me_s, slab_each, ys_rows.at[pl.ds(g0, n), pl.ds(0, NY - KY)],
            )
        )

    repeat(ZL * YL // 16, density_step)
    for lo, hi in ((0, 128), (128, 256), (256, 324)):
        v = jnp.zeros((24, hi - lo), jnp.float32)
        for i in range(H):
            w = jnp.broadcast_to(weight[i : i + 1, 0:1], (24, hi - lo))
            v += w * (occ_h[i, :, lo:hi] + block_mixing * occ_r[i, :, lo:hi])
        occ_out[:, lo:hi] = mask[:, lo:hi] * v

    for c, chunk in enumerate(CHUNKS):
        g0, n = chunk[0], len(chunk)
        width = slice(0, 128 * n)
        arrive(phase(c, 1), zin.at[pl.ds(g0, n)])

        def z_pack(z):
            at = pl.ds(pl.multiple_of(z * 64, 64), 64)
            for g in chunk:
                lanes = slice(128 * (g - g0), 128 * (g - g0) + 128)
                zh[at, lanes], zl[at, lanes] = split(
                    regroup([zin[g, ky] for ky in range(KY)], z)
                )

        repeat(ZL, z_pack)
        zu[:, width] = dot3(tz0[...], tz1[...], zh[:, width], zl[:, width])

        def z_filter(z):
            at = pl.ds(pl.multiple_of(z * 64, 64), 64)
            v = zu[at, width] * fac[at, 128 * g0 : 128 * (g0 + n)]
            zh[at, width], zl[at, width] = split(v)

        repeat(ZL, z_filter)
        zu[:, width] = dot3(tz2[...], tz3[...], zh[:, width], zl[:, width])

        def z_unpack(ky):
            for g in chunk:
                lanes = slice(128 * (g - g0), 128 * (g - g0) + 128)
                planes = [zu[64 * z : 64 * z + 64, lanes] for z in range(ZL)]
                zout[g, ky] = regroup(planes, ky)

        repeat(KY, z_unpack)
        done.append(
            exchange(
                phase(c, 2),
                lambda q, g0=g0, n=n: zout_rows.at[pl.ds(g0, n), :, q],
                lambda m, g0=g0, n=n: yb_rows.at[pl.ds(g0, n), pl.ds(m * KY, KY)],
                me_s, slab_each, zout_rows.at[pl.ds(g0, n), :, pl.ds(0, SLABS - 1)],
            )
        )

    for c, chunk in enumerate(CHUNKS):
        g0, n = chunk[0], len(chunk)
        arrive(phase(c, 2), yb.at[pl.ds(g0, n)])
        y = jnp.concatenate([yb[g] for g in chunk], axis=1)
        y = dot3(tx2[...], tx3[...], *split(y))
        for g in chunk:
            lanes = slice(128 * (g - g0), 128 * (g - g0) + 128)
            yo[:, g] = y[:, lanes].reshape(PENCILS, YL, 128)
        done.append(
            exchange(
                phase(c, 3),
                lambda q, g0=g0, n=n: yo.at[q, pl.ds(g0, n)],
                lambda m, g0=g0, n=n: xi.at[m, pl.ds(g0, n)],
                me_p, pencil_each, yo.at[pl.ds(0, PENCILS - 1), pl.ds(g0, n)],
            )
        )

    for c, chunk in enumerate(CHUNKS):
        g0, g1 = chunk[0], chunk[-1] + 1
        n = g1 - g0
        tile = slice(128 * c, 128 * c + 64 * n)
        rows = slice(64 * g0, 64 * g1)
        arrive(phase(c, 3), xi.at[:, pl.ds(g0, n)])

        def end_step(z):
            at = pl.ds(pl.multiple_of(z * YL, YL), YL)
            h = regroup([xi[b, g] for g in chunk for b in range(PENCILS)], z)
            hh, hl = split(h[:, : 64 * n])
            v = dm[at, :] + grid_mixing * dot3(hh, hl, tx0[rows, :], tx1[rows, :])
            if c == len(CHUNKS) - 1:
                out[at, :] = v
            else:
                dm[at, :] = v

        repeat(ZL, end_step)
    for finish in done:
        finish()


def body(
    density_history, residual_history, occupancy_history, occupancy_residual, species, slot_count
):
    mask = block_mask(species, slot_count)
    qx = real_basis(NX)
    qz = real_basis(NZ)
    qz = qz.reshape(NZ, SLABS, ZL).transpose(0, 2, 1).reshape(NZ, NZ)
    tables = two_parts(qx) + two_parts(qx.T) + two_parts(qz) + two_parts(qz.T)
    f32 = jnp.float32
    bf16 = jnp.bfloat16
    vmem = pl.BlockSpec(memory_space=pltpu.VMEM)
    hbm = pl.BlockSpec(memory_space=pl.ANY)
    rows = ZL * YL
    new_density, new_occupancy = pl.pallas_call(
        kernel,
        in_specs=[hbm, hbm, vmem, vmem, vmem] + [hbm] * 8,
        out_specs=[vmem, vmem],
        out_shape=[
            jax.ShapeDtypeStruct((rows, NX), f32),
            jax.ShapeDtypeStruct(mask.shape, f32),
        ],
        scratch_shapes=[
            pltpu.VMEM((H, rows, NX), f32),
            pltpu.VMEM((H, rows, NX), f32),
        ]
        + [pltpu.VMEM((NX, NX), bf16)] * 4
        + [pltpu.VMEM((NZ, NZ), bf16)] * 4
        + [
            pltpu.VMEM((1, 1, 128), f32),
            pltpu.VMEM((EIGHT, 1, 128), f32),
            pltpu.VMEM((1, 1, 128), f32),
            pltpu.VMEM((SLABS // 2, 1, 128), f32),
            pltpu.VMEM((8, 128), f32),
            pltpu.VMEM((rows, NX), bf16),
            pltpu.VMEM((rows, NX), bf16),
            pltpu.VMEM((rows, 128 * len(CHUNKS)), f32),
            pltpu.VMEM((PENCILS, LT, YL, 128), f32),
            pltpu.VMEM((PENCILS, LT, YL, 128), f32),
            pltpu.VMEM((LT, NY, 128), f32),
            pltpu.VMEM((LT, KY, SLABS, 128), f32),
            pltpu.VMEM((NZ, 256), bf16),
            pltpu.VMEM((NZ, 256), bf16),
            pltpu.VMEM((NZ, 128 * LT), f32),
            pltpu.VMEM((NZ, 256), f32),
            pltpu.VMEM((LT, KY, SLABS, 128), f32),
            pltpu.VMEM((LT, NY, 128), f32),
            pltpu.VMEM((PENCILS, LT, YL, 128), f32),
            pltpu.VMEM((PENCILS, LT, YL, 128), f32),
            pltpu.VMEM((rows, NX), f32),
            pltpu.SemaphoreType.DMA((ZL,)),
            pltpu.SemaphoreType.DMA((9,)),
            pltpu.SemaphoreType.DMA((2 + 4 * len(CHUNKS),)),
            pltpu.SemaphoreType.DMA((2 + 4 * len(CHUNKS),)),
        ],
        compiler_params=pltpu.CompilerParams(
            collective_id=0, has_side_effects=True, vmem_limit_bytes=56 * 2**20
        ),
    )(
        residual_history.reshape(H, rows, NX),
        density_history.reshape(H, rows, NX),
        occupancy_history,
        occupancy_residual,
        mask,
        *tables,
    )
    return (new_density.reshape(ZL, YL, NX), new_occupancy)


def solution(mesh):
    torus = Mesh(
        mesh.devices.reshape(8, 4, 2, mesh.shape["pencil"]),
        ("slab_0", "slab_1", "slab_2", "pencil"),
    )
    placed = (
        P(None, SLAB, "pencil", None),
        P(None, SLAB, "pencil", None),
        P(None, SLAB_PENCIL, None),
        P(None, SLAB_PENCIL, None),
        P(SLAB_PENCIL),
        P(SLAB_PENCIL),
    )
    return jax.shard_map(
        body,
        mesh=torus,
        in_specs=placed,
        out_specs=(P(SLAB, "pencil", None), P(SLAB_PENCIL, None)),
        check_vma=False,
    )
```

time: 106 us -> 85.5 us (0.81)
  Pallas kernels: 99.3 us -> 79 us
    pallas_call x1, Pallas kernels: 99.3 us -> 79 us  [body(): pl.pallas_call(kernel, in_specs=[hbm, hbm, vmem, vmem, vmem] + [hbm] * 8,...]
where the time goes in v2:
time: 85.5 us; the launch traced here: 85.3 us
  Pallas kernels  79 us (92%)
  local copies, waits for them, and re-layouts  3.6 us (4%)
  other arithmetic  1.37 us (2%)
  between operations  1.29 us (2%)
    pallas_call x1, Pallas kernels, body(): pl.pallas_call(kernel, in_specs=[hbm, hbm, vmem, vmem, vmem] + [hbm] * 8,...  79 us
    unnamed x2, local copies, waits for them, and re-layouts  3.6 us

profile of v2, /device:TPU:1, one launch (start us, length us, event | category | flops | bytes accessed | tf_op | source)
XLA Modules:
  0.0 85.3 jit_solution(1417149819948563592)
XLA Ops:
  1.3 0.7 fusion.9
  2.0 0.7 and_convert_fusion.mask
  2.7 79.0 %shard_map.149 = (f32[640,320]{1,0:T(8,128)}, f32[24,324]{1,0:T(8,128)}) custom-call(f32[7,640,320]{2,1,0:T(8,128)} %bitcast.5, f32[7,640,320]{2,1,0:T(8,128)} %bitcast.6, f32[7,24,324]{2,1,0:T(8,128)} %occ_h.1, f32[7,24,324]{2,1,0:T(8,128)} %occ_r.1, f32[24,324]{1,0:T(8,128)} %and_convert_fusion.mask, bf16[320,320]{1,0:T(8,128)(2,1)} %constant.53.clone.t0, ...), custom_call_target="tpu_custom_call" | custom-call | tf_op jit(solution)/shard_map/pallas_call | solution.py:454
  81.7 2.2 %copy.19 = f32[8,80,320]{2,1,0:T(8,128)} copy(f32[8,80,320]{2,1,0:T(8,128)} %bitcast.7) | data formatting | bytes 1638400
  83.9 1.4 %copy.20 = f32[24,324]{1,0:T(8,128)} copy(f32[24,324]{1,0:T(8,128)} %get-tuple-element.11) | data formatting | bytes 62208
  (2 shorter events, 0.0 us)

commit v3 on v2

--- a/solution.py
+++ b/solution.py
@@ -54,22 +54,6 @@
     return upper, lower
 
 
-def block_mask(species, slot_count):
-    live = jnp.arange(species.shape[0], dtype=jnp.int32) < slot_count[0]
-    orbitals = jnp.zeros_like(species)
-    for species_index, orbital_number in enumerate(species_orbitals):
-        orbitals = orbitals + orbital_number * (species == species_index).astype(jnp.int32)
-    entry = jnp.arange(ORBITALS * ORBITALS, dtype=jnp.int32)
-    row_index = entry // ORBITALS
-    column_index = entry % ORBITALS
-    inside = (
-        (row_index[None, :] < orbitals[:, None])
-        & (column_index[None, :] < orbitals[:, None])
-        & live[:, None]
-    )
-    return inside.astype(jnp.float32)
-
-
 def split(value):
     upper = value.astype(jnp.bfloat16)
     lower = (value - upper.astype(jnp.float32)).astype(jnp.bfloat16)
@@ -99,8 +83,9 @@
 
 
 def kernel(
-    res, den, occ_h, occ_r, mask, t0, t1, t2, t3, t4, t5, t6, t7,
-    out, occ_out,
+    species, slot_count, res, den, occ_history, occ_residual, t0, t1, t2, t3, t4, t5, t6, t7,
+    part_out, last_out, occ_out,
+    occ_h, occ_r, mask,
     r7, d7, tx0, tx1, tx2, tx3, tz0, tz1, tz2, tz3,
     row_mine, row_pencil, row_group, row_slab, weight,
     mh, ml, hs, xs, yin, ys, zin, zh, zl, fac, zu, zout, yb, yo, xi, dm,
@@ -155,6 +140,9 @@
     ):
         tables.append(pltpu.make_async_copy(a, b, table_sem.at[n]))
     tables.append(pltpu.make_async_copy(den, d7, table_sem.at[8]))
+    tables.append(pltpu.make_async_copy(occ_history, occ_h, table_sem.at[9]))
+    occupancy = pltpu.make_async_copy(occ_residual, occ_r, load_sem.at[ZL])
+    occupancy.start()
 
     barrier = pltpu.get_barrier_semaphore()
     def greet(q, device):
@@ -170,6 +158,25 @@
 
     def pad(v):
         return jnp.concatenate([v, jnp.zeros((8, 128 - v.shape[1]), v.dtype)], axis=1)
+
+    lane = lanes_of((8, 128))
+    sub = lax.broadcasted_iota(jnp.int32, (8, 128), 0)
+    for r0 in range(0, 24, 8):
+        orbitals = jnp.zeros((8, 128), jnp.int32)
+        for r in range(8):
+            kind = species[r0 + r]
+            number = jnp.int32(0)
+            for index, value in enumerate(species_orbitals):
+                number = jnp.where(kind == index, value, number)
+            number = jnp.where(r0 + r < slot_count[0], number, 0)
+            orbitals = jnp.where(sub == r, number, orbitals)
+        for t in range(3):
+            entry = lane + 128 * t
+            column = entry
+            for row in range(1, ORBITALS):
+                column = jnp.where(entry >= ORBITALS * row, entry - ORBITALS * row, column)
+            inside = (entry < ORBITALS * orbitals) & (column < orbitals)
+            mask[r0 : r0 + 8, 128 * t : 128 * t + 128] = jnp.where(inside, 1.0, 0.0)
 
     def block_step(r, acc):
         at = pl.ds(pl.multiple_of(r * 8, 8), 8)
@@ -180,6 +187,7 @@
             acc = add_products(acc, v if hi - lo == 128 else [pad(x) for x in v])
         return tuple(acc)
 
+    occupancy.wait()
     block = lax.fori_loop(0, 3, block_step, (zero,) * len(PAIRS))
     cells = NX * NY * NZ
     scale = cells / (100.0 * SLABS * PENCILS * mask.shape[0])
@@ -199,8 +207,6 @@
     for c in tables:
         c.start()
 
-    lane = lanes_of((8, 128))
-    sub = lax.broadcasted_iota(jnp.int32, (8, 128), 0)
     spread = zero
     for n0 in range(0, len(PAIRS), 8):
         tile = zero
@@ -331,23 +337,22 @@
             v += w320[i] * d7[i, at]
         dm[at, :] = v
 
-    ys_rows = ys.reshape(LT, NY, 1, 128)
-    zin_rows = zin.reshape(LT, KY, SLABS, 1, 128)
-    zout_rows = zout.reshape(LT, KY, SLABS, 1, 128)
-    yb_rows = yb.reshape(LT, NY, 1, 128)
+    ys_rows, zin_rows, zout_rows, yb_rows = (
+        ref.reshape(LT * NY, 1, 128) for ref in (ys, zin, zout, yb)
+    )
     for c, chunk in enumerate(CHUNKS):
         g0, n = chunk[0], len(chunk)
         arrive(phase(c, 0), yin.at[:, pl.ds(g0, n)])
         y = jnp.concatenate([yin[:, g].reshape(NY, 128) for g in chunk], axis=1)
         y = dot3(tx0[...], tx1[...], *split(y))
-        for g in chunk:
-            ys[g] = y[:, 128 * (g - g0) : 128 * (g - g0) + 128]
+        for g in range(n):
+            ys[pl.ds(g0 * NY + g, NY, stride=n), :] = y[:, 128 * g : 128 * g + 128]
         done.append(
             exchange(
                 phase(c, 1),
-                lambda q, g0=g0, n=n: ys_rows.at[pl.ds(g0, n), pl.ds(q * KY, KY)],
-                lambda m, g0=g0, n=n: zin_rows.at[pl.ds(g0, n), :, m],
-                me_s, slab_each, ys_rows.at[pl.ds(g0, n), pl.ds(0, NY - KY)],
+                lambda q, g0=g0, n=n: ys_rows.at[pl.ds(g0 * NY + q * (KY * n), KY * n)],
+                lambda m, g0=g0, n=n: zin_rows.at[pl.ds(g0 * NY + m * (KY * n), KY * n)],
+                me_s, slab_each, ys_rows.at[pl.ds(g0 * NY, (NY - KY) * n)],
             )
         )
 
@@ -362,15 +367,16 @@
     for c, chunk in enumerate(CHUNKS):
         g0, n = chunk[0], len(chunk)
         width = slice(0, 128 * n)
-        arrive(phase(c, 1), zin.at[pl.ds(g0, n)])
+        arrive(phase(c, 1), zin.at[pl.ds(g0 * NY, n * NY)])
 
         def z_pack(z):
             at = pl.ds(pl.multiple_of(z * 64, 64), 64)
-            for g in chunk:
-                lanes = slice(128 * (g - g0), 128 * (g - g0) + 128)
-                zh[at, lanes], zl[at, lanes] = split(
-                    regroup([zin[g, ky] for ky in range(KY)], z)
-                )
+            for g in range(n):
+                lanes = slice(128 * g, 128 * g + 128)
+                lines = [
+                    zin[pl.ds(g0 * NY + ky * n + g, SLABS, stride=KY * n), :] for ky in range(KY)
+                ]
+                zh[at, lanes], zl[at, lanes] = split(regroup(lines, z))
 
         repeat(ZL, z_pack)
         zu[:, width] = dot3(tz0[...], tz1[...], zh[:, width], zl[:, width])
@@ -384,25 +390,27 @@
         zu[:, width] = dot3(tz2[...], tz3[...], zh[:, width], zl[:, width])
 
         def z_unpack(ky):
-            for g in chunk:
-                lanes = slice(128 * (g - g0), 128 * (g - g0) + 128)
+            for g in range(n):
+                lanes = slice(128 * g, 128 * g + 128)
                 planes = [zu[64 * z : 64 * z + 64, lanes] for z in range(ZL)]
-                zout[g, ky] = regroup(planes, ky)
+                at = pl.ds(g0 * NY + ky * n + g, SLABS, stride=KY * n)
+                zout[at, :] = regroup(planes, ky)
 
         repeat(KY, z_unpack)
         done.append(
             exchange(
                 phase(c, 2),
-                lambda q, g0=g0, n=n: zout_rows.at[pl.ds(g0, n), :, q],
-                lambda m, g0=g0, n=n: yb_rows.at[pl.ds(g0, n), pl.ds(m * KY, KY)],
-                me_s, slab_each, zout_rows.at[pl.ds(g0, n), :, pl.ds(0, SLABS - 1)],
+                lambda q, g0=g0, n=n: zout_rows.at[pl.ds(g0 * NY + q * (KY * n), KY * n)],
+                lambda m, g0=g0, n=n: yb_rows.at[pl.ds(g0 * NY + m * (KY * n), KY * n)],
+                me_s, slab_each, zout_rows.at[pl.ds(g0 * NY, (NY - KY) * n)],
             )
         )
 
     for c, chunk in enumerate(CHUNKS):
         g0, n = chunk[0], len(chunk)
-        arrive(phase(c, 2), yb.at[pl.ds(g0, n)])
-        y = jnp.concatenate([yb[g] for g in chunk], axis=1)
+        arrive(phase(c, 2), yb.at[pl.ds(g0 * NY, n * NY)])
+        y = [yb[pl.ds(g0 * NY + g, NY, stride=n), :] for g in range(n)]
+        y = jnp.concatenate(y, axis=1)
         y = dot3(tx2[...], tx3[...], *split(y))
         for g in chunk:
             lanes = slice(128 * (g - g0), 128 * (g - g0) + 128)
@@ -419,29 +427,47 @@
     for c, chunk in enumerate(CHUNKS):
         g0, g1 = chunk[0], chunk[-1] + 1
         n = g1 - g0
-        tile = slice(128 * c, 128 * c + 64 * n)
         rows = slice(64 * g0, 64 * g1)
         arrive(phase(c, 3), xi.at[:, pl.ds(g0, n)])
+        if c == len(CHUNKS) - 1:
+            break
 
         def end_step(z):
             at = pl.ds(pl.multiple_of(z * YL, YL), YL)
             h = regroup([xi[b, g] for g in chunk for b in range(PENCILS)], z)
             hh, hl = split(h[:, : 64 * n])
-            v = dm[at, :] + grid_mixing * dot3(hh, hl, tx0[rows, :], tx1[rows, :])
-            if c == len(CHUNKS) - 1:
-                out[at, :] = v
-            else:
-                dm[at, :] = v
+            dm[at, :] += grid_mixing * dot3(hh, hl, tx0[rows, :], tx1[rows, :])
 
         repeat(ZL, end_step)
+        if c == len(CHUNKS) - 2:
+            part = pltpu.make_async_copy(dm, part_out, load_sem.at[ZL + 1])
+            part.start()
+    last = pltpu.make_async_copy(xi.at[:, pl.ds(g0, n)], last_out, load_sem.at[ZL + 2])
+    last.start()
     for finish in done:
         finish()
+    part.wait()
+    last.wait()
+
+
+def last_kernel(part, last, tx0, tx1, occ, out, occ_out):
+    n = last.shape[1]
+    for half in range(2):
+        at = slice(half * YL, half * YL + YL)
+        z = 2 * pl.program_id(0) + half
+        h = regroup([last[b, g] for g in range(n) for b in range(PENCILS)], z)
+        rows = slice(NX - 64 * n, NX)
+        hh, hl = split(h[:, : 64 * n])
+        out[at, :] = part[at, :] + grid_mixing * dot3(hh, hl, tx0[rows, :], tx1[rows, :])
+
+    @pl.when(pl.program_id(0) == 0)
+    def _():
+        occ_out[...] = occ[...]
 
 
 def body(
     density_history, residual_history, occupancy_history, occupancy_residual, species, slot_count
 ):
-    mask = block_mask(species, slot_count)
     qx = real_basis(NX)
     qz = real_basis(NZ)
     qz = qz.reshape(NZ, SLABS, ZL).transpose(0, 2, 1).reshape(NZ, NZ)
@@ -450,16 +476,23 @@
     bf16 = jnp.bfloat16
     vmem = pl.BlockSpec(memory_space=pltpu.VMEM)
     hbm = pl.BlockSpec(memory_space=pl.ANY)
+    smem = pl.BlockSpec(memory_space=pltpu.SMEM)
+    slots, entries = occupancy_history.shape[1:]
     rows = ZL * YL
-    new_density, new_occupancy = pl.pallas_call(
+    last_tiles = len(CHUNKS[-1])
+    part, last, occupancy = pl.pallas_call(
         kernel,
-        in_specs=[hbm, hbm, vmem, vmem, vmem] + [hbm] * 8,
-        out_specs=[vmem, vmem],
+        in_specs=[smem, smem] + [hbm] * 12,
+        out_specs=[hbm, hbm, vmem],
         out_shape=[
             jax.ShapeDtypeStruct((rows, NX), f32),
-            jax.ShapeDtypeStruct(mask.shape, f32),
+            jax.ShapeDtypeStruct((PENCILS, last_tiles, YL, 128), f32),
+            jax.ShapeDtypeStruct((slots, entries), f32),
         ],
         scratch_shapes=[
+            pltpu.VMEM((H, slots, entries), f32),
+            pltpu.VMEM((H, slots, entries), f32),
+            pltpu.VMEM((slots, 384), f32),
             pltpu.VMEM((H, rows, NX), f32),
             pltpu.VMEM((H, rows, NX), f32),
         ]
@@ -476,19 +509,19 @@
             pltpu.VMEM((rows, 128 * len(CHUNKS)), f32),
             pltpu.VMEM((PENCILS, LT, YL, 128), f32),
             pltpu.VMEM((PENCILS, LT, YL, 128), f32),
-            pltpu.VMEM((LT, NY, 128), f32),
-            pltpu.VMEM((LT, KY, SLABS, 128), f32),
+            pltpu.VMEM((LT * NY, 128), f32),
+            pltpu.VMEM((LT * NY, 128), f32),
             pltpu.VMEM((NZ, 256), bf16),
             pltpu.VMEM((NZ, 256), bf16),
             pltpu.VMEM((NZ, 128 * LT), f32),
             pltpu.VMEM((NZ, 256), f32),
-            pltpu.VMEM((LT, KY, SLABS, 128), f32),
-            pltpu.VMEM((LT, NY, 128), f32),
+            pltpu.VMEM((LT * NY, 128), f32),
+            pltpu.VMEM((LT * NY, 128), f32),
             pltpu.VMEM((PENCILS, LT, YL, 128), f32),
             pltpu.VMEM((PENCILS, LT, YL, 128), f32),
             pltpu.VMEM((rows, NX), f32),
-            pltpu.SemaphoreType.DMA((ZL,)),
-            pltpu.SemaphoreType.DMA((9,)),
+            pltpu.SemaphoreType.DMA((ZL + 3,)),
+            pltpu.SemaphoreType.DMA((10,)),
             pltpu.SemaphoreType.DMA((2 + 4 * len(CHUNKS),)),
             pltpu.SemaphoreType.DMA((2 + 4 * len(CHUNKS),)),
         ],
@@ -496,13 +529,33 @@
             collective_id=0, has_side_effects=True, vmem_limit_bytes=56 * 2**20
         ),
     )(
+        species,
+        slot_count,
         residual_history.reshape(H, rows, NX),
         density_history.reshape(H, rows, NX),
         occupancy_history,
         occupancy_residual,
-        mask,
         *tables,
     )
+    new_density, new_occupancy = pl.pallas_call(
+        last_kernel,
+        grid=(ZL // 2,),
+        in_specs=[
+            pl.BlockSpec((2 * YL, NX), lambda z: (z, 0)),
+            pl.BlockSpec(last.shape, lambda z: (0, 0, 0, 0)),
+            pl.BlockSpec((NX, NX), lambda z: (0, 0)),
+            pl.BlockSpec((NX, NX), lambda z: (0, 0)),
+            pl.BlockSpec((slots, entries), lambda z: (0, 0)),
+        ],
+        out_specs=[
+            pl.BlockSpec((2 * YL, NX), lambda z: (z, 0)),
+            pl.BlockSpec((slots, entries), lambda z: (0, 0)),
+        ],
+        out_shape=[
+            jax.ShapeDtypeStruct((rows, NX), f32),
+            jax.ShapeDtypeStruct((slots, entries), f32),
+        ],
+    )(part, last, tables[0], tables[1], occupancy)
     return (new_density.reshape(ZL, YL, NX), new_occupancy)
 
 

time: 85.5 us -> 83.1 us (0.972)
  local copies, waits for them, and re-layouts: 3.6 us -> 0 us
  Pallas kernels: 79 us -> 81.7 us
  other arithmetic: 1.37 us -> 0 us
    unnamed x2 -> x0, local copies, waits for them, and re-layouts: 3.6 us -> none
    pallas_call x1 -> x2, Pallas kernels: 79 us -> 81.7 us  [the longest x1 77.1 us: body(): pl.pallas_call(kernel, in_specs=[smem, smem] + [hbm] * 12, out_specs=[hbm...]
where the time goes in v3:
time: 83.1 us; the launch traced here: 83 us
  Pallas kernels  81.7 us (98%)
  between operations  1.29 us (2%)
    pallas_call x1, Pallas kernels, body(): pl.pallas_call(kernel, in_specs=[smem, smem] + [hbm] * 12, out_specs=[hbm...  77.1 us
    pallas_call x1, Pallas kernels, body(): pl.pallas_call(last_kernel, grid=(ZL // 2,), in_specs=[pl.BlockSpec((2 *...  4.62 us

profile of v3, /device:TPU:1, one launch (start us, length us, event | category | flops | bytes accessed | tf_op | source)
XLA Modules:
  0.0 83.0 jit_solution(2979704449767957425)
XLA Ops:
  1.3 77.1 %shard_map.149 = (f32[640,320]{1,0:T(8,128)}, f32[4,2,80,128]{3,2,1,0:T(8,128)}, f32[24,324]{1,0:T(8,128)}) custom-call(s32[24]{0:T(128)} %species.1, s32[1]{0:T(128)S(6)} %copy.16.slot_count, f32[7,640,320]{2,1,0:T(8,128)} %bitcast.3, f32[7,640,320]{2,1,0:T(8,128)} %bitcast.4, f32[7,24,324]{2,1,0:T(8,128)} %occ_history.1, f32[7,24,324]{2,1,0:T(8,128)} %occ_residual.1, ...), custom_call_target="tpu_custom_call" | custom-call | tf_op jit(solution)/shard_map/pallas_call | solution.py:483
  78.4 4.6 %shard_map.150 = (f32[640,320]{1,0:T(8,128)}, f32[24,324]{1,0:T(8,128)}) custom-call(f32[640,320]{1,0:T(8,128)} %get-tuple-element.7.part, f32[4,2,80,128]{3,2,1,0:T(8,128)} %get-tuple-element.8.last, bf16[320,320]{1,0:T(8,128)(2,1)} %constant.16.clone.t0.tx0, bf16[320,320]{1,0:T(8,128)(2,1)} %constant.17.clone.t1.tx1, f32[24,324]{1,0:T(8,128)} %get-tuple-element.9.occ), custom_call_target="tpu_custom_call" | custom-call | tf_op jit(solution)/shard_map/pallas_call | solution.py:540

commit v4 on v3

--- a/solution.py
+++ b/solution.py
@@ -317,13 +317,24 @@
             for g in chunk:
                 xs[b, g] = regroup(planes, 4 * (g - g0) + b)
 
-        repeat(PENCILS, x_pack)
+        def pack_each(act):
+            ready = None
+            for r in (2, 1, 3, 0):
+                q = lax.rem(me_p + r, PENCILS)
+                x_pack(q)
+                if ready is not None:
+                    act(*ready)
+                ready = (q, (s0, s1, s2, q))
+
+        if c > 0:
+            repeat(PENCILS, x_pack)
         done.append(
             exchange(
                 phase(c, 0),
                 lambda q, g0=g0, n=n: xs.at[q, pl.ds(g0, n)],
                 lambda m, g0=g0, n=n: yin.at[m, pl.ds(g0, n)],
-                me_p, pencil_each, xs.at[pl.ds(0, PENCILS - 1), pl.ds(g0, n)],
+                me_p, pencil_each if c > 0 else pack_each,
+                xs.at[pl.ds(0, PENCILS - 1), pl.ds(g0, n)],
             )
         )
 
@@ -452,13 +463,16 @@
 
 def last_kernel(part, last, tx0, tx1, occ, out, occ_out):
     n = last.shape[1]
-    for half in range(2):
-        at = slice(half * YL, half * YL + YL)
-        z = 2 * pl.program_id(0) + half
+    rows = slice(NX - 64 * n, NX)
+
+    def plane_step(plane):
+        at = pl.ds(pl.multiple_of(plane * YL, YL), YL)
+        z = 4 * pl.program_id(0) + plane
         h = regroup([last[b, g] for g in range(n) for b in range(PENCILS)], z)
-        rows = slice(NX - 64 * n, NX)
         hh, hl = split(h[:, : 64 * n])
         out[at, :] = part[at, :] + grid_mixing * dot3(hh, hl, tx0[rows, :], tx1[rows, :])
+
+    repeat(4, plane_step)
 
     @pl.when(pl.program_id(0) == 0)
     def _():
@@ -539,16 +553,16 @@
     )
     new_density, new_occupancy = pl.pallas_call(
         last_kernel,
-        grid=(ZL // 2,),
+        grid=(ZL // 4,),
         in_specs=[
-            pl.BlockSpec((2 * YL, NX), lambda z: (z, 0)),
+            pl.BlockSpec((4 * YL, NX), lambda z: (z, 0)),
             pl.BlockSpec(last.shape, lambda z: (0, 0, 0, 0)),
             pl.BlockSpec((NX, NX), lambda z: (0, 0)),
             pl.BlockSpec((NX, NX), lambda z: (0, 0)),
             pl.BlockSpec((slots, entries), lambda z: (0, 0)),
         ],
         out_specs=[
-            pl.BlockSpec((2 * YL, NX), lambda z: (z, 0)),
+            pl.BlockSpec((4 * YL, NX), lambda z: (z, 0)),
             pl.BlockSpec((slots, entries), lambda z: (0, 0)),
         ],
         out_shape=[

time: 83.1 us -> 83.4 us (level)
  no operation moved by 1% of the time
where the time goes in v4:
time: 83.4 us; the launch traced here: 83.2 us
  Pallas kernels  82 us (98%)
  between operations  1.29 us (2%)
    pallas_call x1, Pallas kernels, body(): pl.pallas_call(kernel, in_specs=[smem, smem] + [hbm] * 12, out_specs=[hbm...  77.1 us
    pallas_call x1, Pallas kernels, body(): pl.pallas_call(last_kernel, grid=(ZL // 4,), in_specs=[pl.BlockSpec((4 *...  4.86 us

profile of v4, /device:TPU:1, one launch (start us, length us, event | category | flops | bytes accessed | tf_op | source)
XLA Modules:
  0.0 83.2 jit_solution(7608240700857350652)
XLA Ops:
  1.3 77.1 %shard_map.149 = (f32[640,320]{1,0:T(8,128)}, f32[4,2,80,128]{3,2,1,0:T(8,128)}, f32[24,324]{1,0:T(8,128)}) custom-call(s32[24]{0:T(128)} %species.1, s32[1]{0:T(128)S(6)} %copy.16.slot_count, f32[7,640,320]{2,1,0:T(8,128)} %bitcast.3, f32[7,640,320]{2,1,0:T(8,128)} %bitcast.4, f32[7,24,324]{2,1,0:T(8,128)} %occ_history.1, f32[7,24,324]{2,1,0:T(8,128)} %occ_residual.1, ...), custom_call_target="tpu_custom_call" | custom-call | tf_op jit(solution)/shard_map/pallas_call | solution.py:497
  78.4 4.9 %shard_map.150 = (f32[640,320]{1,0:T(8,128)}, f32[24,324]{1,0:T(8,128)}) custom-call(f32[640,320]{1,0:T(8,128)} %get-tuple-element.7.part, f32[4,2,80,128]{3,2,1,0:T(8,128)} %get-tuple-element.8.last, bf16[320,320]{1,0:T(8,128)(2,1)} %constant.16.clone.t0.tx0, bf16[320,320]{1,0:T(8,128)(2,1)} %constant.17.clone.t1.tx1, f32[24,324]{1,0:T(8,128)} %get-tuple-element.9.occ), custom_call_target="tpu_custom_call" | custom-call | tf_op jit(solution)/shard_map/pallas_call | solution.py:554
